TPU v7x, 256 devices: a whole 4x4x8 slice. The times are simulated.
256 devices in a mesh: row: 32 (over y, z_hi, core), col: 8 (over x, z_lo).
Axes of the slice: x: 4, y: 4, z: 8 (z_hi: 4, z_lo: 2; z = z_hi * 2 + z_lo), core: 2. Of those that a mesh axis runs over, the one named last changes fastest.
Arguments:
- vectors: float32 [8192, 32768], P(('row', 'col')), may hold values from -6 to 6
- reflectors: float32 [6, 128, 32768], P(None, 'col', 'row')
- factors: float32 [6, 128, 128], replicated, as said below
Outputs:
- transformed: float32 [8192, 32768], P('col', 'row')
Inputs may be any that keep to these rules, and one draw needn't show every extreme that they name: factors[k] is upper triangular, and its inverse equals the strict upper part of reflectors[k] reflectors[k]^T plus half of that product's diagonal, so each panel is orthogonal.
All inputs are finite; a program needn't handle non-finite values.
Results may differ from a plain program's by a relative error of at most 0.0001.
Values sent between devices are 32-bit elements; how exact they have to be, the bound alone decides.
A program may use at most 128 MiB of HBM per device.

v0:
```python
import jax
import jax.numpy as jnp
from jax import lax
from jax.sharding import Mesh
from jax.sharding import PartitionSpec as P

ROW = ("row_0", "row_1", "row_2")
ROW_COL = ("row_0", "row_1", "row_2", "col")


def split_up(value, dim, length):
    dims = value.shape
    parts = value.reshape(*dims[:dim], length, dims[dim] // length, *dims[dim + 1 :])
    return jnp.moveaxis(parts, dim, 0)


def sum_at_owner(value, axis, dim):
    parts = split_up(value, dim, lax.axis_size(axis))
    arrived = lax.all_to_all(parts, axis, split_axis=0, concat_axis=0, tiled=True)
    return arrived.sum(axis=0)


def summed_rows(value, axes, dim):
    far, near = axes
    parts = split_up(value, dim, lax.axis_size(far))
    nearer = sum_at_owner(parts, near, dim + 1)
    arrived = lax.all_to_all(nearer, far, split_axis=0, concat_axis=0, tiled=True)
    return arrived.sum(axis=0)


def padded_to(lines, length):
    spare = -len(lines) % length
    return jnp.pad(lines, [(0, spare)] + [(0, 0)] * (lines.ndim - 1))


def sent_to_all(value, axis):
    copies = jnp.broadcast_to(value, (lax.axis_size(axis), *value.shape))
    return lax.all_to_all(copies, axis, split_axis=0, concat_axis=0, tiled=True)


def laid_out(parts, dim):
    parts = jnp.moveaxis(parts, 0, dim)
    dims = parts.shape
    return parts.reshape(*dims[:dim], dims[dim] * dims[dim + 1], *dims[dim + 2 :])


def whole_of(value, axes, dim):
    far, near = axes
    first = sent_to_all(value, far)
    parts = jnp.swapaxes(sent_to_all(first, near), 0, 1)
    return laid_out(parts.reshape(-1, *value.shape), dim)


def sum_by_parts(value, axes):
    own = summed_rows(padded_to(value, lax.axis_size(axes[0]) * lax.axis_size(axes[1])), axes, 0)
    whole = whole_of(own, axes, 0)
    return whole[: len(value)].reshape(value.shape)


def in_one(arrays, axis):
    ends = [0]
    for a in arrays:
        ends.append(ends[-1] + a.size)
    subtotal = sum_by_parts(jnp.concatenate([a.ravel() for a in arrays]), axis)
    return tuple((subtotal[b:e].reshape(a.shape) for a, b, e in zip(arrays, ends, ends[1:])))


def product(left, right):
    return jnp.dot(left, right, precision=lax.Precision.HIGHEST, preferred_element_type=jnp.float32)


def against(left, right):
    return lax.dot_general(
        left,
        right,
        (((1,), (1,)), ((), ())),
        precision=lax.Precision.HIGHEST,
        preferred_element_type=jnp.float32,
    )


def on_device(vectors, reflectors, factors):
    local_count, length = vectors.shape
    row_count = lax.axis_size(ROW)
    col_count = lax.axis_size("col")
    piece_length = length // row_count
    shaped = vectors.reshape(local_count, row_count, piece_length)
    arrived = lax.all_to_all(
        lax.all_to_all(shaped, ROW, split_axis=1, concat_axis=0, tiled=True),
        "col",
        split_axis=0,
        concat_axis=1,
        tiled=True,
    )
    arrived = arrived.reshape(row_count // col_count, local_count, col_count, piece_length)
    current = jnp.swapaxes(arrived, 1, 2).reshape(-1, piece_length)
    panels = lax.all_gather(reflectors, "col", axis=1, tiled=True)
    count = panels.shape[0]
    width = panels.shape[1]
    stacked_all = panels.reshape(count * width, piece_length)
    partial_value = against(current, stacked_all)
    pair_list = []
    for first in range(count):
        for second in range(first + 1, count):
            pair_list.append(against(panels[first], panels[second]))
    crossed = jnp.stack(pair_list, axis=0)
    projection, crossed = in_one((partial_value, crossed), (("row_0", "row_1"), "row_2"))
    lookup = {}
    position = 0
    for first in range(count):
        for second in range(first + 1, count):
            lookup[first, second] = crossed[position]
            position = position + 1
    blocks_of = {}
    for second in range(count):
        blocks_of[second, second] = factors[second]
        for first in range(second - 1, -1, -1):
            total = jnp.zeros((width, width), jnp.float32)
            for middle in range(first + 1, second + 1):
                total = total + product(lookup[first, middle], blocks_of[middle, second])
            blocks_of[first, second] = -product(factors[first], total)
    block_rows = []
    for first in range(count):
        pieces = []
        for second in range(count):
            if second < first:
                pieces.append(jnp.zeros((width, width), jnp.float32))
            else:
                pieces.append(blocks_of[first, second])
        block_rows.append(jnp.concatenate(pieces, axis=1))
    factor_all = jnp.concatenate(block_rows, axis=0)
    update = against(projection, factor_all)
    current = current - product(update, stacked_all)
    return current


def solution(mesh):
    finer = Mesh(
        mesh.devices.reshape(4, 4, 2, mesh.shape["col"]), ("row_0", "row_1", "row_2", "col")
    )
    placed = (P(ROW_COL, None), P(None, "col", ROW), P())
    return jax.shard_map(
        on_device, mesh=finer, in_specs=placed, out_specs=P("col", ROW), check_vma=False
    )
```

profile of v0, /device:TPU:5, one launch (start us, length us, event | category | flops | bytes accessed | tf_op | source)
XLA Modules:
  0.0 494.7 jit_solution(6361075090651696708)
XLA Ops:
  6.5 4.8 copy.63
  11.3 12.0 %all-to-all-start = ((f32[32,32,1024]{2,0,1:T(8,128)}), f32[32,32,1024]{2,0,1:T(8,128)}, u32[]{:S(2)}, u32[]{:S(2)}) async-start(f32[32,32,1024]{2,0,1:T(8,128)} %bitcast.309), calls=%async_computation | async-start | bytes 8388608 | tf_op jit(solution)/shard_map/all_to_all | solution.py:89
  24.0 134.0 %all-to-all-done = f32[32,32,1024]{2,0,1:T(8,128)} async-done(((f32[32,32,1024]{2,0,1:T(8,128)}), f32[32,32,1024]{2,0,1:T(8,128)}, u32[]{:S(2)}, u32[]{:S(2)}) %all-to-all-start) | async-done | bytes 4194336 | tf_op jit(solution)/shard_map/all_to_all | solution.py:89
  158.0 8.5 %copy.39 = f32[1024,1,1024]{2,1,0:T(1,128)} copy(f32[1024,1,1024]{2,0,1:T(8,128)} %bitcast.2) | data formatting | bytes 8388608 | tf_op jit(solution)/shard_map/all_to_all | solution.py:89
  166.5 5.1 %all-to-all-start.1 = ((f32[1024,1,1024]{2,1,0:T(1,128)}), f32[1024,1,1024]{2,1,0:T(1,128)}, u32[]{:S(2)}, u32[]{:S(2)}) async-start(f32[1024,1,1024]{2,1,0:T(1,128)} %copy.39), calls=%async_computation.1 | async-start | bytes 8388608 | tf_op jit(solution)/shard_map/all_to_all | solution.py:88
  171.7 3.2 all-gather.2.cloned.1.call-done
  174.8 2.5 fusion.26
  177.4 2.4 fusion.25
  179.8 2.4 fusion.24
  196.6 22.2 %all-to-all-done.1 = f32[1024,1,1024]{2,1,0:T(1,128)} async-done(((f32[1024,1,1024]{2,1,0:T(1,128)}), f32[1024,1,1024]{2,1,0:T(1,128)}, u32[]{:S(2)}, u32[]{:S(2)}) %all-to-all-start.1) | async-done | bytes 4194336 | tf_op jit(solution)/shard_map/all_to_all | solution.py:88
  218.9 3.2 copy.52
  222.7 2.0 copy-done.1
  224.7 12.0 %fusion.138 = f32[1024,768]{1,0:T(8,128)} fusion(f32[1024,1024]{1,0:T(8,128)S(1)} %bitcast.307, f32[768,1024]{1,0:T(8,128)S(1)} %bitcast.305), kind=kOutput, calls=%fused_computation.217 | convolution fusion | flops 9663676416 | bytes 10485760 | tf_op jit(solution)/shard_map/dot_general | solution.py:73
  236.7 4.4 reshape.98
  241.1 4.4 pad_maximum_fusion
  245.5 5.9 %reshape_reshape.4 = f32[16,2,32256]{2,1,0:T(2,128)} reshape(f32[1032192]{0:T(1024)} %pad_maximum_fusion) | data formatting | bytes 8257536 | tf_op jit(solution)/shard_map/reshape;reshape | solution.py:13
  251.4 3.0 copy.42
  254.4 8.6 %all_to_all.61 = f32[2,16,32256]{2,1,0:T(8,128)} all-to-all(f32[2,16,32256]{2,1,0:T(8,128)S(1)} %copy.42), channel_id=1, replica_groups=mesh['row_0'=4,'row_1'=4,'row_2'=2,'col'=8] {'row_2'}, dimensions={0} | all-to-all | bytes 8257536 | tf_op jit(solution)/shard_map/all_to_all | solution.py:19
  263.0 4.0 reduce_sum.18
  267.0 3.0 all_to_all.50
  270.0 56.4 %all_to_all.62 = f32[16,1,32256]{2,1,0:T(1,128)} all-to-all(f32[16,1,32256]{2,1,0:T(1,128)S(1)} %all_to_all.50), channel_id=1, replica_groups=mesh['row_0'=4,'row_1'=4,'row_2'=2,'col'=8] {'row_0','row_1'}, dimensions={0} | all-to-all | bytes 4128768 | tf_op jit(solution)/shard_map/all_to_all | solution.py:27
  326.3 3.5 reduce_sum.19
  329.8 3.3 broadcast_in_dim.6
  333.2 6.6 %all-to-all-start.4 = ((f32[16,1,32256]{2,1,0:T(1,128)}), f32[16,1,32256]{2,1,0:T(1,128)}, u32[]{:S(2)}, u32[]{:S(2)}) async-start(f32[16,1,32256]{2,1,0:T(1,128)} %broadcast_in_dim.6), calls=%async_computation.4 | async-start | bytes 4128768 | tf_op jit(solution)/shard_map/all_to_all | solution.py:38
  351.3 29.4 %all-to-all-done.4 = f32[16,1,32256]{2,1,0:T(1,128)} async-done(((f32[16,1,32256]{2,1,0:T(1,128)}), f32[16,1,32256]{2,1,0:T(1,128)}, u32[]{:S(2)}, u32[]{:S(2)}) %all-to-all-start.4) | async-done | bytes 2064416 | tf_op jit(solution)/shard_map/all_to_all | solution.py:38
  380.7 1.7 copy.64
  382.7 19.7 %all_to_all.63 = f32[2,16,32256]{2,1,0:T(8,128)S(1)} all-to-all(f32[2,16,32256]{2,1,0:T(8,128)S(1)} %broadcast_in_dim.7), channel_id=1, replica_groups=mesh['row_0'=4,'row_1'=4,'row_2'=2,'col'=8] {'row_2'}, dimensions={0} | all-to-all | bytes 8257536 | tf_op jit(solution)/shard_map/all_to_all | solution.py:38
  402.4 5.1 %copy.43 = f32[16,2,32256]{2,1,0:T(2,128)} copy(f32[16,2,32256]{2,0,1:T(8,128)S(1)} %bitcast.312) | data formatting | bytes 8257536 | tf_op jit(solution)/shard_map/transpose | solution.py:50
  407.6 6.3 %slice.188 = f32[8064,128]{1,0:T(8,128)} reshape(f32[16,2,32256]{2,1,0:T(2,128)} %copy.43) | data formatting | bytes 8257536 | tf_op jit(solution)/shard_map/slice | solution.py:112
  422.2 6.6 %slice.185 = f32[1344,768]{1,0:T(8,128)} reshape(f32[16,2,32256]{2,1,0:T(2,128)} %copy.43) | data formatting | bytes 8257536 | tf_op jit(solution)/shard_map/slice | solution.py:65
  467.8 8.2 %fusion = f32[1024,768]{1,0:T(8,128)S(1)} fusion(f32[768,768]{0,1:T(8,128)S(1)} %maximum_dynamic-update-slice_fusion, f32[1344,768]{1,0:T(8,128)S(1)} %copy-done.4), kind=kOutput, calls=%fused_computation.2 | convolution fusion | flops 7247757312 | bytes 8650752 | tf_op jit(solution)/shard_map/dot_general | solution.py:73
  476.1 11.6 %convolution_subtract_fusion = f32[1024,1024]{1,0:T(8,128)} fusion(f32[1024,1024]{1,0:T(8,128)S(1)} %bitcast.308, f32[1024,768]{1,0:T(8,128)S(1)} %fusion, f32[768,1024]{1,0:T(8,128)S(1)} %bitcast.306), kind=kOutput, calls=%fused_computation.5 | convolution fusion | flops 9664724992 | bytes 14680064 | tf_op jit(solution)/shard_map/dot_general | solution.py:69
  (123 shorter events, 74.3 us)
Async XLA Ops:
  11.3 146.7 %all-to-all-start = ((f32[32,32,1024]{2,0,1:T(8,128)}), f32[32,32,1024]{2,0,1:T(8,128)}, u32[]{:S(2)}, u32[]{:S(2)}) async-start(f32[32,32,1024]{2,0,1:T(8,128)} %bitcast.309), calls=%async_computation | async-start | bytes 8388608 | tf_op jit(solution)/shard_map/all_to_all | solution.py:89
  23.3 151.5 %all-gather.2.cloned.1.call-start = ((), (), s32[]{:S(2)}) async-start(), calls=%async_computation.6 | async-start | bytes 3538944 | tf_op jit(solution)/shard_map/all_gather | solution.py:97
  166.5 52.3 %all-to-all-start.1 = ((f32[1024,1,1024]{2,1,0:T(1,128)}), f32[1024,1,1024]{2,1,0:T(1,128)}, u32[]{:S(2)}, u32[]{:S(2)}) async-start(f32[1024,1,1024]{2,1,0:T(1,128)} %copy.39), calls=%async_computation.1 | async-start | bytes 8388608 | tf_op jit(solution)/shard_map/all_to_all | solution.py:88
  174.8 7.4 %copy-start = (f32[6,128,1024]{2,1,0:T(8,128)S(1)}, f32[6,128,1024]{2,1,0:T(8,128)}, u32[]{:S(2)}) copy-start(f32[6,128,1024]{2,1,0:T(8,128)} %all-gather.2.cloned.1.call-done) | copy-start | bytes 9437188
  222.7 2.0 copy-start.1
  329.8 9.9 %copy-start.3 = (f32[6,128,128]{2,1,0:T(8,128)S(1)}, f32[6,128,128]{2,1,0:T(8,128)}, u32[]{:S(2)}) copy-start(f32[6,128,128]{2,1,0:T(8,128)} %param.5) | copy-start | bytes 1179652
  333.2 47.5 %all-to-all-start.4 = ((f32[16,1,32256]{2,1,0:T(1,128)}), f32[16,1,32256]{2,1,0:T(1,128)}, u32[]{:S(2)}, u32[]{:S(2)}) async-start(f32[16,1,32256]{2,1,0:T(1,128)} %broadcast_in_dim.6), calls=%async_computation.4 | async-start | bytes 4128768 | tf_op jit(solution)/shard_map/all_to_all | solution.py:38
  428.9 17.6 %copy-start.9 = (f32[128,128]{1,0:T(8,128)S(1)}, f32[128,128]{1,0:T(8,128)}, u32[]{:S(2)}) copy-start(f32[128,128]{1,0:T(8,128)} %fusion.42) | copy-start | bytes 196612
  432.2 25.1 %copy-start.8 = (f32[128,128]{1,0:T(8,128)S(1)}, f32[128,128]{1,0:T(8,128)}, u32[]{:S(2)}) copy-start(f32[128,128]{1,0:T(8,128)} %fusion.48) | copy-start | bytes 196612
  438.3 25.2 %copy-start.7 = (f32[128,128]{1,0:T(8,128)S(1)}, f32[128,128]{1,0:T(8,128)}, u32[]{:S(2)}) copy-start(f32[128,128]{1,0:T(8,128)} %fusion.54) | copy-start | bytes 196612
  440.8 25.1 %copy-start.5 = (f32[768,768]{0,1:T(8,128)S(1)}, f32[768,768]{0,1:T(8,128)}, u32[]{:S(2)}) copy-start(f32[768,768]{0,1:T(8,128)} %bitcast_dynamic-update-slice_fusion.12) | copy-start | bytes 7077892
  440.8 25.1 %copy-start.6 = (f32[128,128]{1,0:T(8,128)S(1)}, f32[128,128]{1,0:T(8,128)}, u32[]{:S(2)}) copy-start(f32[128,128]{1,0:T(8,128)} %fusion.65) | copy-start | bytes 196612
  445.4 22.0 %copy-start.14 = (f32[1,128,128]{1,2,0:T(8,128)S(1)}, f32[1,128,128]{1,2,0:T(8,128)}, u32[]{:S(2)}) copy-start(f32[1,128,128]{1,2,0:T(8,128)} %copy.55) | copy-start | bytes 196612
  448.9 18.6 %copy-start.13 = (f32[1,128,128]{1,2,0:T(8,128)S(1)}, f32[1,128,128]{1,2,0:T(8,128)}, u32[]{:S(2)}) copy-start(f32[1,128,128]{1,2,0:T(8,128)} %copy.56) | copy-start | bytes 196612
  451.5 16.2 %copy-start.12 = (f32[1,128,128]{1,2,0:T(8,128)S(1)}, f32[1,128,128]{1,2,0:T(8,128)}, u32[]{:S(2)}) copy-start(f32[1,128,128]{1,2,0:T(8,128)} %copy.57) | copy-start | bytes 196612
  453.9 13.8 %copy-start.11 = (f32[1,128,128]{1,2,0:T(8,128)S(1)}, f32[1,128,128]{1,2,0:T(8,128)}, u32[]{:S(2)}) copy-start(f32[1,128,128]{1,2,0:T(8,128)} %copy.58) | copy-start | bytes 196612
  457.3 10.5 %copy-start.10 = (f32[1,128,128]{1,2,0:T(8,128)S(1)}, f32[1,128,128]{1,2,0:T(8,128)}, u32[]{:S(2)}) copy-start(f32[1,128,128]{1,2,0:T(8,128)} %copy.59) | copy-start | bytes 196612
  460.0 7.8 %copy-start.4 = (f32[1344,768]{1,0:T(8,128)S(1)}, f32[1344,768]{1,0:T(8,128)}, u32[]{:S(2)}) copy-start(f32[1344,768]{1,0:T(8,128)} %slice.185) | copy-start | bytes 12386308
  467.8 8.2 %copy-start.2 = (f32[4,8,32,1024]{3,2,1,0:T(8,128)S(1)}, f32[4,8,32,1024]{3,2,1,0:T(8,128)}, u32[]{:S(2)}) copy-start(f32[4,8,32,1024]{3,2,1,0:T(8,128)} %copy-done.1) | copy-start | bytes 12582916
Sparse Core Ops, SparseCore 0:
  25.9 148.8 all-gather.1
where the time goes:
time: 502 us; the launch traced here: 495 us
  waiting for transfers between devices  189 us (38%)
  matrix products  100 us (20%)
  blocking collectives  84.7 us (17%)
  local copies, waits for them, and re-layouts  70.7 us (14%)
  starting transfers between devices  23.7 us (5%)
  between operations  14.2 us (3%)
  other arithmetic  11.9 us (2%)
    all_to_all x1, waiting for transfers between devices, on_device(): lax.all_to_all(shaped, ROW, split_axis=1, concat_axis=0, tiled=True)  134 us
    dot_general x51, matrix products, product(): jnp.dot(left, right, precision=lax.Precision.HIGHEST, preferred_element_t...  58.1 us
    all_to_all x1, blocking collectives, summed_rows(): lax.all_to_all(nearer, far, split_axis=0, concat_axis=0, tiled=True)  56.4 us
    dot_general x17, matrix products, against(): lax.dot_general(left, right, (((1,), (1,)), ((), ())), precision=lax.Prec...  42 us
    all_to_all x1, waiting for transfers between devices, sent_to_all(): return lax.all_to_all(copies, axis, split_axis=0, concat_axis=0, tiled=True)  29.4 us
    all_to_all x1, waiting for transfers between devices, on_device(): lax.all_to_all(lax.all_to_all(shaped, ROW, split_axis=1, concat_axis=0, t...  22.2 us
    all_to_all x1, blocking collectives, sent_to_all(): return lax.all_to_all(copies, axis, split_axis=0, concat_axis=0, tiled=True)  19.7 us
    unnamed x55, local copies, waits for them, and re-layouts  17.9 us
  transfers between devices with their start and end apart: 4, of which 4 were waited for; matrix products, arithmetic and copies ran while one was open for 8% of the time, Pallas kernels for 0%

commit v1 on v0

--- a/solution.py
+++ b/solution.py
@@ -1,6 +1,8 @@
 import jax
 import jax.numpy as jnp
 from jax import lax
+from jax.experimental import pallas as pl
+from jax.experimental.pallas import tpu as pltpu
 from jax.sharding import Mesh
 from jax.sharding import PartitionSpec as P
 
@@ -79,21 +81,109 @@
     )
 
 
+def place(row_far, row_near, col):
+    return (row_far, row_near // 2, row_near % 2, col)
+
+
+def exchange_kernel(vec, out, held, sent_a, came_a, sent_b, came_b, local):
+    y, near = lax.axis_index("row_0"), lax.axis_index("row_1") * 2 + lax.axis_index("row_2")
+    col = lax.axis_index("col")
+    slot = (near % 4) * 8 + col
+    rows = vec.shape[0]
+    piece = vec.shape[1] // 32
+    mesh_id = pl.DeviceIdType.MESH
+    barrier = pltpu.get_barrier_semaphore()
+    for k in range(1, 4):
+        pl.semaphore_signal(barrier, inc=1, device_id=place((y + k) % 4, near, col), device_id_type=mesh_id)
+    for k in range(4):
+        for w in range(8):
+            pl.semaphore_signal(barrier, inc=1, device_id=place(y, w, k * 2 + near // 4), device_id_type=mesh_id)
+    for w in range(4):
+        for c in range(8):
+            pl.semaphore_signal(barrier, inc=1, device_id=place(y, (col % 2) * 4 + w, c), device_id_type=mesh_id)
+    pl.semaphore_wait(barrier, 3 + 64)
+
+    def columns(far, w):
+        return vec.at[:, pl.ds(pl.multiple_of((far * 8 + w) * piece, piece), piece)]
+
+    def first(k, w):
+        far = (y + k) % 4
+        return pltpu.make_async_remote_copy(
+            src_ref=columns(far, w), dst_ref=held.at[k - 1, w],
+            send_sem=sent_a.at[k - 1, w], recv_sem=came_a.at[k - 1, w],
+            device_id=place(far, near, col), device_id_type=mesh_id,
+        )
+
+    def second(k, w, start):
+        origin = (y - k) % 4
+        source = held.at[k - 1, w] if k else columns(y, w)
+        target = out.at[pl.ds(pl.multiple_of(slot * rows, rows), rows), :]
+        there = origin * 2 + near // 4
+        mine = jnp.logical_and(w == near, there == col)
+
+        @pl.when(mine)
+        def _():
+            copy = pltpu.make_async_copy(source, target, local)
+            copy.start() if start else copy.wait()
+
+        @pl.when(jnp.logical_not(mine))
+        def _():
+            copy = pltpu.make_async_remote_copy(
+                src_ref=source, dst_ref=target, send_sem=sent_b.at[k, w], recv_sem=came_b.at[slot],
+                device_id=place(y, w, there), device_id_type=mesh_id,
+            )
+            copy.start() if start else copy.wait_send()
+
+    for i in range(8):
+        for k in (1, 3, 2):
+            first(k, near ^ i).start()
+    for i in range(8):
+        second(0, near ^ i, True)
+    for i in range(8):
+        for k in (1, 3, 2):
+            first(k, near ^ i).wait_recv()
+            second(k, near ^ i, True)
+    for s in range(32):
+        relayed_here = jnp.logical_and(near == (col % 2) * 4 + s // 8, col == s % 8)
+
+        @pl.when(jnp.logical_not(relayed_here))
+        def _():
+            block = out.at[pl.ds(s * rows, rows), :]
+            pltpu.make_async_remote_copy(
+                src_ref=block, dst_ref=block, send_sem=sent_b.at[0, 0], recv_sem=came_b.at[s],
+                device_id=place(y, near, col), device_id_type=mesh_id,
+            ).wait_recv()
+    for k in range(4):
+        for w in range(8):
+            second(k, w, False)
+            if k:
+                first(k, w).wait_send()
+
+
+def exchanged(vectors):
+    rows, length = vectors.shape
+    piece = length // 32
+    return pl.pallas_call(
+        exchange_kernel,
+        out_shape=jax.ShapeDtypeStruct((rows * 32, piece), jnp.float32),
+        in_specs=[pl.BlockSpec(memory_space=pl.ANY)],
+        out_specs=pl.BlockSpec(memory_space=pl.ANY),
+        scratch_shapes=[
+            pltpu.VMEM((3, 8, rows, piece), jnp.float32),
+            pltpu.SemaphoreType.DMA((3, 8)),
+            pltpu.SemaphoreType.DMA((3, 8)),
+            pltpu.SemaphoreType.DMA((4, 8)),
+            pltpu.SemaphoreType.DMA((32,)),
+            pltpu.SemaphoreType.DMA,
+        ],
+        compiler_params=pltpu.CompilerParams(collective_id=1, has_side_effects=True),
+        cost_estimate=pl.CostEstimate(flops=10**9, bytes_accessed=2**23, transcendentals=0),
+    )(vectors)
+
+
 def on_device(vectors, reflectors, factors):
-    local_count, length = vectors.shape
-    row_count = lax.axis_size(ROW)
-    col_count = lax.axis_size("col")
-    piece_length = length // row_count
-    shaped = vectors.reshape(local_count, row_count, piece_length)
-    arrived = lax.all_to_all(
-        lax.all_to_all(shaped, ROW, split_axis=1, concat_axis=0, tiled=True),
-        "col",
-        split_axis=0,
-        concat_axis=1,
-        tiled=True,
-    )
-    arrived = arrived.reshape(row_count // col_count, local_count, col_count, piece_length)
-    current = jnp.swapaxes(arrived, 1, 2).reshape(-1, piece_length)
+    piece_length = vectors.shape[1] // lax.axis_size(ROW)
+    current = exchanged(vectors)
     panels = lax.all_gather(reflectors, "col", axis=1, tiled=True)
     count = panels.shape[0]
     width = panels.shape[1]

time: 502 us -> 476 us (0.948)
  the two profiles are of different devices: /device:TPU:5 before, /device:TPU:39 now
where the time goes in v1:
time: 476 us; the launch traced here: 468 us
  Pallas kernels  123 us (26%)
  blocking collectives  93.4 us (20%)
  matrix products  89.3 us (19%)
  waiting for transfers between devices  82 us (17%)
  local copies, waits for them, and re-layouts  52.1 us (11%)
  between operations  14.6 us (3%)
  other arithmetic  9.77 us (2%)
  starting transfers between devices  4.76 us (1%)
    pallas_call x1, Pallas kernels, exchanged(): pl.pallas_call(exchange_kernel, out_shape=jax.ShapeDtypeStruct((rows * 32...  123 us
    all_to_all x1, blocking collectives, summed_rows(): lax.all_to_all(nearer, far, split_axis=0, concat_axis=0, tiled=True)  77.7 us
    dot_general x51, matrix products, product(): jnp.dot(left, right, precision=lax.Precision.HIGHEST, preferred_element_t...  58.1 us
    all_gather x1, waiting for transfers between devices, on_device(): panels = lax.all_gather(reflectors, 'col', axis=1, tiled=True)  46.5 us
    all_to_all x1, waiting for transfers between devices, sent_to_all(): return lax.all_to_all(copies, axis, split_axis=0, concat_axis=0, tiled=True)  34.7 us
    dot_general x17, matrix products, against(): lax.dot_general(left, right, (((1,), (1,)), ((), ())), precision=lax.Prec...  31.2 us
    unnamed x54, local copies, waits for them, and re-layouts  12.7 us
  transfers between devices with their start and end apart: 2, of which 2 were waited for; matrix products, arithmetic and copies ran while one was open for 2% of the time, Pallas kernels for 26%

profile of v1, /device:TPU:39, one launch (start us, length us, event | category | flops | bytes accessed | tf_op | source)
XLA Modules:
  0.0 468.4 jit_solution(5211649741351170019)
XLA Ops:
  7.3 122.5 %shard_map.37 = f32[1024,1024]{1,0:T(8,128)} custom-call(f32[32,32768]{1,0:T(8,128)} %vec.1), custom_call_target="tpu_custom_call" | custom-call | flops 1000000000 | bytes 8388608 | tf_op jit(solution)/shard_map/pallas_call | solution.py:166
  129.8 46.5 %all-gather.2.cloned.1.call-done = f32[6,128,1024]{2,1,0:T(8,128)} async-done(((f32[6,16,1024]{2,1,0:T(8,128)}), f32[6,128,1024]{2,1,0:T(8,128)}) %all-gather.2.cloned.1.call-update) | async-done | bytes 3145744 | tf_op jit(solution)/shard_map/all_gather | solution.py:187
  176.3 14.2 %fusion.138 = f32[1024,768]{1,0:T(8,128)} fusion(f32[1024,1024]{1,0:T(8,128)} %shard_map.37, f32[768,1024]{1,0:T(8,128)} %bitcast.288), kind=kOutput, calls=%fused_computation.216 | convolution fusion | flops 9663676416 | bytes 10485760 | tf_op jit(solution)/shard_map/dot_general | solution.py:75
  190.6 5.1 %reshape.85 = f32[786432]{0:T(1024)} reshape(f32[1024,768]{1,0:T(8,128)} %fusion.138) | data formatting | bytes 6291456 | tf_op jit(solution)/shard_map/reshape | solution.py:66
  204.5 2.3 pad_maximum_fusion
  206.8 5.9 %reshape_reshape.4 = f32[16,2,32256]{2,1,0:T(2,128)} reshape(f32[1032192]{0:T(1024)} %pad_maximum_fusion) | data formatting | bytes 8257536 | tf_op jit(solution)/shard_map/reshape;reshape | solution.py:15
  212.7 3.0 copy.24
  215.7 8.3 %all_to_all.28 = f32[2,16,32256]{2,1,0:T(8,128)} all-to-all(f32[2,16,32256]{2,1,0:T(8,128)S(1)} %copy.24), channel_id=1, replica_groups=mesh['row_0'=4,'row_1'=4,'row_2'=2,'col'=8] {'row_2'}, dimensions={0} | all-to-all | bytes 8257536 | tf_op jit(solution)/shard_map/all_to_all | solution.py:21
  224.0 4.0 reduce_sum.18
  228.0 3.0 all_to_all.19
  231.0 77.7 %all_to_all.29 = f32[16,1,32256]{2,1,0:T(1,128)} all-to-all(f32[16,1,32256]{2,1,0:T(1,128)S(1)} %all_to_all.19), channel_id=1, replica_groups=mesh['row_0'=4,'row_1'=4,'row_2'=2,'col'=8] {'row_0','row_1'}, dimensions={0} | all-to-all | bytes 4128768 | tf_op jit(solution)/shard_map/all_to_all | solution.py:29
  308.7 3.5 reduce_sum.19
  312.1 3.3 broadcast_in_dim.6
  315.5 4.8 %all-to-all-start.2 = ((f32[16,1,32256]{2,1,0:T(1,128)}), f32[16,1,32256]{2,1,0:T(1,128)}, u32[]{:S(2)}, u32[]{:S(2)}) async-start(f32[16,1,32256]{2,1,0:T(1,128)} %broadcast_in_dim.6), calls=%async_computation.2 | async-start | bytes 4128768 | tf_op jit(solution)/shard_map/all_to_all | solution.py:40
  321.0 1.6 copy.34
  322.6 1.6 copy.35
  324.1 1.6 copy.36
  327.3 1.6 copy.38
  328.8 1.6 copy.39
  331.8 34.7 %all-to-all-done.2 = f32[16,1,32256]{2,1,0:T(1,128)} async-done(((f32[16,1,32256]{2,1,0:T(1,128)}), f32[16,1,32256]{2,1,0:T(1,128)}, u32[]{:S(2)}, u32[]{:S(2)}) %all-to-all-start.2) | async-done | bytes 2064416 | tf_op jit(solution)/shard_map/all_to_all | solution.py:40
  366.6 1.7 copy.41
  368.6 7.3 %all_to_all.30 = f32[2,16,32256]{2,1,0:T(8,128)S(1)} all-to-all(f32[2,16,32256]{2,1,0:T(8,128)S(1)} %broadcast_in_dim.7), channel_id=1, replica_groups=mesh['row_0'=4,'row_1'=4,'row_2'=2,'col'=8] {'row_2'}, dimensions={0} | all-to-all | bytes 8257536 | tf_op jit(solution)/shard_map/all_to_all | solution.py:40
  375.9 5.2 %copy.25 = f32[16,2,32256]{2,1,0:T(2,128)} copy(f32[16,2,32256]{2,0,1:T(8,128)S(1)} %bitcast.291) | data formatting | bytes 8257536 | tf_op jit(solution)/shard_map/transpose | solution.py:52
  381.1 6.3 %slice.188 = f32[8064,128]{1,0:T(8,128)} reshape(f32[16,2,32256]{2,1,0:T(2,128)} %copy.25) | data formatting | bytes 8257536 | tf_op jit(solution)/shard_map/slice | solution.py:202
  387.4 1.7 fusion.31
  389.1 1.7 fusion.42
  390.8 1.7 fusion.48
  392.4 1.7 fusion.54
  394.1 1.7 fusion.65
  395.7 6.5 %slice.185 = f32[1344,768]{1,0:T(8,128)} reshape(f32[16,2,32256]{2,1,0:T(2,128)} %copy.25) | data formatting | bytes 8257536 | tf_op jit(solution)/shard_map/slice | solution.py:67
  441.2 8.3 %fusion = f32[1024,768]{1,0:T(8,128)S(1)} fusion(f32[768,768]{0,1:T(8,128)S(1)} %maximum_dynamic-update-slice_fusion, f32[1344,768]{1,0:T(8,128)S(1)} %copy-done.3), kind=kOutput, calls=%fused_computation.1 | convolution fusion | flops 7247757312 | bytes 8650752 | tf_op jit(solution)/shard_map/dot_general | solution.py:75
  449.5 11.6 %convolution_subtract_fusion = f32[1024,1024]{1,0:T(8,128)} fusion(f32[1024,1024]{1,0:T(8,128)S(1)} %copy-done.1, f32[1024,768]{1,0:T(8,128)S(1)} %fusion, f32[768,1024]{1,0:T(8,128)S(1)} %bitcast.289), kind=kOutput, calls=%fused_computation.4 | convolution fusion | flops 9664724992 | bytes 14680064 | tf_op jit(solution)/shard_map/dot_general | solution.py:71
  (116 shorter events, 51.9 us)
Async XLA Ops:
  6.5 169.8 %all-gather.2.cloned.1.call-start = ((), (), s32[]{:S(2)}) async-start(), calls=%async_computation.4 | async-start | bytes 3538944 | tf_op jit(solution)/shard_map/all_gather | solution.py:187
  190.6 5.1 %copy-start = (f32[6,128,1024]{2,1,0:T(8,128)S(1)}, f32[6,128,1024]{2,1,0:T(8,128)}, u32[]{:S(2)}) copy-start(f32[6,128,1024]{2,1,0:T(8,128)} %all-gather.2.cloned.1.call-done) | copy-start | bytes 9437188
  201.0 3.5 copy-start.4
  312.1 8.1 %copy-start.2 = (f32[6,128,128]{2,1,0:T(8,128)S(1)}, f32[6,128,128]{2,1,0:T(8,128)}, u32[]{:S(2)}) copy-start(f32[6,128,128]{2,1,0:T(8,128)} %param.5) | copy-start | bytes 1179652
  315.5 51.1 %all-to-all-start.2 = ((f32[16,1,32256]{2,1,0:T(1,128)}), f32[16,1,32256]{2,1,0:T(1,128)}, u32[]{:S(2)}, u32[]{:S(2)}) async-start(f32[16,1,32256]{2,1,0:T(1,128)} %broadcast_in_dim.6), calls=%async_computation.2 | async-start | bytes 4128768 | tf_op jit(solution)/shard_map/all_to_all | solution.py:40
  402.2 17.6 %copy-start.9 = (f32[128,128]{1,0:T(8,128)S(1)}, f32[128,128]{1,0:T(8,128)}, u32[]{:S(2)}) copy-start(f32[128,128]{1,0:T(8,128)} %fusion.42) | copy-start | bytes 196612
  405.5 25.0 %copy-start.8 = (f32[128,128]{1,0:T(8,128)S(1)}, f32[128,128]{1,0:T(8,128)}, u32[]{:S(2)}) copy-start(f32[128,128]{1,0:T(8,128)} %fusion.48) | copy-start | bytes 196612
  411.6 25.2 %copy-start.7 = (f32[128,128]{1,0:T(8,128)S(1)}, f32[128,128]{1,0:T(8,128)}, u32[]{:S(2)}) copy-start(f32[128,128]{1,0:T(8,128)} %fusion.54) | copy-start | bytes 196612
  414.1 25.1 %copy-start.5 = (f32[768,768]{0,1:T(8,128)S(1)}, f32[768,768]{0,1:T(8,128)}, u32[]{:S(2)}) copy-start(f32[768,768]{0,1:T(8,128)} %bitcast_dynamic-update-slice_fusion.12) | copy-start | bytes 7077892
  414.1 25.1 %copy-start.6 = (f32[128,128]{1,0:T(8,128)S(1)}, f32[128,128]{1,0:T(8,128)}, u32[]{:S(2)}) copy-start(f32[128,128]{1,0:T(8,128)} %fusion.65) | copy-start | bytes 196612
  418.7 22.0 %copy-start.14 = (f32[1,128,128]{1,2,0:T(8,128)S(1)}, f32[1,128,128]{1,2,0:T(8,128)}, u32[]{:S(2)}) copy-start(f32[1,128,128]{1,2,0:T(8,128)} %copy.35) | copy-start | bytes 196612
  422.3 18.6 %copy-start.13 = (f32[1,128,128]{1,2,0:T(8,128)S(1)}, f32[1,128,128]{1,2,0:T(8,128)}, u32[]{:S(2)}) copy-start(f32[1,128,128]{1,2,0:T(8,128)} %copy.36) | copy-start | bytes 196612
  424.8 16.2 %copy-start.12 = (f32[1,128,128]{1,2,0:T(8,128)S(1)}, f32[1,128,128]{1,2,0:T(8,128)}, u32[]{:S(2)}) copy-start(f32[1,128,128]{1,2,0:T(8,128)} %copy.37) | copy-start | bytes 196612
  427.3 13.8 %copy-start.11 = (f32[1,128,128]{1,2,0:T(8,128)S(1)}, f32[1,128,128]{1,2,0:T(8,128)}, u32[]{:S(2)}) copy-start(f32[1,128,128]{1,2,0:T(8,128)} %copy.38) | copy-start | bytes 196612
  430.6 10.5 %copy-start.10 = (f32[1,128,128]{1,2,0:T(8,128)S(1)}, f32[1,128,128]{1,2,0:T(8,128)}, u32[]{:S(2)}) copy-start(f32[1,128,128]{1,2,0:T(8,128)} %copy.39) | copy-start | bytes 196612
  433.4 7.8 %copy-start.3 = (f32[1344,768]{1,0:T(8,128)S(1)}, f32[1344,768]{1,0:T(8,128)}, u32[]{:S(2)}) copy-start(f32[1344,768]{1,0:T(8,128)} %slice.185) | copy-start | bytes 12386308
  441.2 8.3 %copy-start.1 = (f32[1024,1024]{1,0:T(8,128)S(1)}, f32[1024,1024]{1,0:T(8,128)}, u32[]{:S(2)}) copy-start(f32[1024,1024]{1,0:T(8,128)} %shard_map.37) | copy-start | bytes 12582916
Sparse Core Ops, SparseCore 0:
  9.1 167.1 all-gather.1

commit v2 on v0

v2 whole, which is shorter than its diff:
```python
import jax
import jax.numpy as jnp
from jax import lax
from jax.experimental import pallas as pl
from jax.experimental.pallas import tpu as pltpu
from jax.sharding import PartitionSpec as P

F32 = jnp.float32
BF16 = jnp.bfloat16
MESH = pl.DeviceIdType.MESH
CHUNKS = 4
NT = (((1,), (1,)), ((), ()))
NN = (((1,), (0,)), ((), ()))


def halves(value):
    high = value.astype(BF16)
    return high, (value - high.astype(F32)).astype(BF16)


def dot3(left, right, dims):
    def one(a, b):
        return lax.dot_general(a, b, dims, preferred_element_type=F32)

    return one(left[0], right[0]) + (one(left[0], right[1]) + one(left[1], right[0]))


def part(index, size):
    return pl.ds(pl.multiple_of(index * size, size), size)


def kernel(
    vec, refl, factors, out,
    x, held, panels, vh, vl, xh, xl, uh, ul, proj, r1, r2, s2, r3, upd,
    gp, g1, gs, g2, gc, gall, th, tl,
    sent_a, came_a, sent_b, came_b, sent_v, came_v, own_v, sent_g, came_g, sent_p, came_p,
):
    row, col = lax.axis_index("row"), lax.axis_index("col")
    y, near = row // 8, row % 8
    zh, core = near // 2, near % 2
    far_x, zl = col // 2, col % 2
    slot = (near % 4) * 8 + col
    upper = near // 4
    count, block, piece = panels.shape
    own = refl.shape[1]
    pending = []

    def at(y_, zh_, core_, col_):
        return (y_ * 8 + zh_ * 2 + core_, col_)

    def in_y(k):
        return at((y + k) % 4, zh, core, col)

    def in_z(k):
        return at(y, (zh + k) % 4, core, col)

    def in_x(k):
        return (row, ((far_x + k) % 4) * 2 + zl)

    twin = at(y, zh, 1 - core, col)

    def remote(src, dst, send_sem, recv_sem, device):
        return pltpu.make_async_remote_copy(
            src_ref=src, dst_ref=dst, send_sem=send_sem, recv_sem=recv_sem,
            device_id=device, device_id_type=MESH,
        )

    def send(*args):
        copy = remote(*args)
        copy.start()
        pending.append(copy)
        return copy

    barrier = pltpu.get_barrier_semaphore()
    greeted = []
    for k in range(4):
        for w in range(8):
            greeted.append((y * 8 + w, k * 2 + upper))
    for w in range(4):
        for c in range(8):
            greeted.append((y * 8 + zl * 4 + w, c))
    for o in range(1, 8):
        greeted.append(at((y + o // 2) % 4, zh, (core + o) % 2, col))
        greeted.append((row, (col + o) % 8))
    for k in range(1, 4):
        greeted.append(in_z(k))
    for device in greeted:
        pl.semaphore_signal(barrier, inc=1, device_id=device, device_id_type=MESH)
    pl.semaphore_wait(barrier, len(greeted))

    mine = panels.at[:, part(col, own), :]
    others = panels.at[:, part(far_x * 2 + 1 - zl, own), :]
    keep = pltpu.make_async_copy(refl, mine, own_v)
    keep.start()
    beside = send(refl, mine, sent_v.at[0], came_v.at[0], (row, far_x * 2 + 1 - zl))
    from_x = [send(refl, mine, sent_v.at[k], came_v.at[k], in_x(k)) for k in (1, 3, 2)]

    first = {}
    for c in range(CHUNKS):
        for k in (1, 3, 2):
            first[c, k] = send(
                vec.at[pl.ds(c * 8, 8), part((y + k) % 4, 8 * piece)], held.at[c, k - 1],
                sent_a.at[c, k - 1], came_a.at[c, k - 1], in_y(k),
            )

    local = zl == upper

    def second(c):
        for k in (0, 1, 3, 2):
            if k:
                first[c, k].wait_recv()
            there = ((y - k) % 4) * 2 + upper
            for flip in range(2):
                for j in (1, 3, 2, 0):
                    to_zh, to_core = (zh + j) % 4, (core + flip) % 2
                    w = to_zh * 2 + to_core
                    if k:
                        source = held.at[c, k - 1, :, part(w, piece)]
                    else:
                        source = vec.at[pl.ds(c * 8, 8), part(y * 8 + w, piece)]
                    target = x.at[c, part(slot, 8), :]
                    copy = remote(source, target, sent_b.at[c], came_b.at[c], at(y, to_zh, to_core, there))
                    if flip or j:
                        copy.start()
                    else:

                        @pl.when(there == col)
                        def _(source=source, target=target):
                            pltpu.make_async_copy(source, target, came_b.at[c]).start()

                        @pl.when(there != col)
                        def _(copy=copy):
                            copy.start()

    second(0)
    beside.wait_recv()
    from_z = [send(others, others, sent_v.at[3 + k], came_v.at[3 + k], in_x(k)) for k in (1, 3, 2)]
    for copy in from_x + from_z:
        copy.wait_recv()
    keep.wait()
    for k in range(count):
        vh[k], vl[k] = halves(panels[k])

    line = col % count
    for d in range(1, 4):
        other = (line + d) % count
        low, high = jnp.minimum(line, other), jnp.maximum(line, other)
        gp[d - 1] = dot3((vh[low], vl[low]), (vh[high], vl[high]), NT)
    lot = block // 8
    step_1 = []
    for o in range(1, 8):
        to_y, to_core = (y + o // 2) % 4, (core + o) % 2
        step_1.append(
            send(
                gp.at[:, part(to_core * 4 + to_y, lot), :], g1.at[o - 1],
                sent_g.at[0, o], came_g.at[0, o], at(to_y, zh, to_core, col),
            )
        )
    second(1)
    for copy in step_1:
        copy.wait_recv()
    total = gp[:, part(core * 4 + y, lot), :]
    for o in range(7):
        total = total + g1[o]
    gs[...] = total
    step_2 = [send(gs, g2.at[k - 1], sent_g.at[1, k], came_g.at[1, k], in_z(k)) for k in (1, 3, 2)]

    def g_col():
        for copy in step_2:
            copy.wait_recv()
        gc[col] = gs[...] + g2[0] + (g2[1] + g2[2])
        return [
            send(gc.at[col], gc.at[col], sent_g.at[2, k], came_g.at[2, k], (row, (col + k) % 8))
            for k in range(1, 8)
        ]

    def g_y(before):
        for copy in before:
            copy.wait_recv()
        lines = part(core * 4 + y, lot)
        gall[:, :, lines, :] = gc[pl.ds(0, count)]
        return [
            send(
                gc.at[pl.ds(0, count)], gall.at[:, :, lines, :],
                sent_g.at[3, k], came_g.at[3, k], in_y(k),
            )
            for k in (1, 3, 2)
        ]

    def g_core(before):
        for copy in before:
            copy.wait_recv()
        lines = part(core, block // 2)
        return send(gall.at[:, :, lines, :], gall.at[:, :, lines, :], sent_g.at[4, 0], came_g.at[4, 0], twin)

    def whole_factor(before):
        before.wait_recv()

        def cross(a, b):
            return gall[a, b - a - 1] if b - a <= 3 else gall[b, count - (b - a) - 1]

        last = count * block
        th[...] = jnp.zeros_like(th)
        tl[...] = jnp.zeros_like(tl)
        for k in range(count - 1, -1, -1):
            inner = halves(factors[k])
            lines, start = pl.ds(k * block, block), (k + 1) * block
            th[lines, lines], tl[lines, lines] = inner
            if start < last:
                rest = pl.ds(start, last - start)
                crossed = jnp.concatenate([cross(k, b) for b in range(k + 1, count)], axis=1)
                met = dot3(halves(crossed), (th[rest, rest], tl[rest, rest]), NN)
                th[lines, rest], tl[lines, rest] = halves(-dot3(inner, halves(met), NN))

    def project(c):
        whole = x.at[c]
        remote(whole, whole, sent_b.at[c], came_b.at[c], (row, col)).wait_recv()
        xh[...], xl[...] = halves(x[c])

        def two(p, carry):
            pair = pl.ds(p * 2, 2)
            right = [ref[pair].reshape(2 * block, piece) for ref in (vh, vl)]
            both = dot3((xh[...], xl[...]), right, NT)
            proj[c, p * 2] = both[:, :block]
            proj[c, p * 2 + 1] = both[:, block:]
            return carry

        lax.fori_loop(0, count // 2, two, 0)
        half = proj.shape[2] // 2
        return [
            send(proj.at[c, :, part(1 - core, half), :], r1.at[c], sent_p.at[c, 0], came_p.at[c, 0], twin)
        ]

    def sum_core(c, before):
        before[0].wait_recv()
        half = proj.shape[2] // 2
        r1[c] = r1[c] + proj[c, :, part(core, half), :]
        return [
            send(
                r1.at[c, :, part((y + k) % 4, half // 4), :], r2.at[c, k - 1],
                sent_p.at[c, k], came_p.at[c, k], in_y(k),
            )
            for k in (1, 3, 2)
        ]

    def sum_y(c, before):
        for copy in before:
            copy.wait_recv()
        s2[c] = r1[c, :, part(y, 32), :] + r2[c, 0] + (r2[c, 1] + r2[c, 2])
        return [
            send(
                s2.at[c, :, part((zh + k) % 4, 8), :], r3.at[c, k - 1],
                sent_p.at[c, 3 + k], came_p.at[c, 3 + k], in_z(k),
            )
            for k in (1, 3, 2)
        ]

    def update(c, before):
        for copy in before:
            copy.wait_recv()
        total = s2[c, :, part(zh, 8), :] + r3[c, 0] + (r3[c, 1] + r3[c, 2])
        flat = jnp.concatenate([total[k] for k in range(count)], axis=1)
        value = dot3(halves(flat), (th[...], tl[...]), NT)
        lines = part((core * 4 + y) * 4 + zh, 8)
        for k in range(count):
            upd[c, k, lines, :] = value[:, k * block : (k + 1) * block]
        ref = upd.at[c, :, lines, :]
        return [send(ref, ref, sent_p.at[c, 6 + k], came_p.at[c, 6 + k], in_z(k)) for k in (1, 3, 2)]

    def all_z(c, before):
        for copy in before:
            copy.wait_recv()
        ref = upd.at[c, :, part(core * 4 + y, 32), :]
        return [send(ref, ref, sent_p.at[c, 9 + k], came_p.at[c, 9 + k], in_y(k)) for k in (1, 3, 2)]

    def all_y(c, before):
        for copy in before:
            copy.wait_recv()
        ref = upd.at[c, :, part(core, 128), :]
        return [send(ref, ref, sent_p.at[c, 13], came_p.at[c, 13], twin)]

    def finish(c, before):
        before[0].wait_recv()
        flat = jnp.concatenate([upd[c, k] for k in range(count)], axis=1)
        uh[...], ul[...] = halves(flat)
        wide = 256

        def tile(t, carry):
            lanes = part(t, wide)
            right = [ref[:, :, lanes].reshape(count * block, wide) for ref in (vh, vl)]
            moved = x[c, :, lanes] - dot3((uh[...], ul[...]), right, NN)
            out[:, c, :, lanes] = moved.reshape(32, 8, wide)
            return carry

        lax.fori_loop(0, piece // wide, tile, 0)

    state = {}
    g = None
    for c in range(CHUNKS + 2):
        if c < CHUNKS:
            state[c] = project(c)
        if c == 0:
            g = g_col()
        if c == 1:
            whole_factor(g)
        if 0 <= c - 1 < CHUNKS:
            state[c - 1] = update(c - 1, state[c - 1])
        if c < CHUNKS:
            state[c] = sum_core(c, state[c])
        if c == 0:
            g = g_y(g)
        if 0 <= c - 2 < CHUNKS:
            state[c - 2] = all_z(c - 2, state[c - 2])
        if c < CHUNKS:
            state[c] = sum_y(c, state[c])
        if c == 0:
            g = g_core(g)
        if c + 2 < CHUNKS:
            second(c + 2)
        if 0 <= c - 2 < CHUNKS:
            state[c - 2] = all_y(c - 2, state[c - 2])
            finish(c - 2, state[c - 2])

    for c in range(CHUNKS):

        @pl.when(local)
        def _():
            some = x.at[c, pl.ds(0, x.shape[1] - 8), :]
            remote(some, some, sent_b.at[c], came_b.at[c], (row, col)).wait_send()

        @pl.when(jnp.logical_not(local))
        def _():
            remote(x.at[c], x.at[c], sent_b.at[c], came_b.at[c], (row, col)).wait_send()

    for copy in pending:
        copy.wait_send()


def on_device(vectors, reflectors, factors):
    count, block = factors.shape[:2]
    rows, length = vectors.shape
    piece = length // 32
    lot = rows * 32 // CHUNKS
    vmem = pltpu.VMEM
    dma = pltpu.SemaphoreType.DMA
    out = pl.pallas_call(
        kernel,
        out_shape=jax.ShapeDtypeStruct((32, CHUNKS, rows // CHUNKS, piece), F32),
        in_specs=[
            pl.BlockSpec(memory_space=pl.ANY),
            pl.BlockSpec(memory_space=pl.ANY),
            pl.BlockSpec(memory_space=vmem),
        ],
        out_specs=pl.BlockSpec(memory_space=vmem),
        scratch_shapes=[
            vmem((CHUNKS, lot, piece), F32),
            vmem((CHUNKS, 3, 8, 8 * piece), F32),
            vmem((count, block, piece), F32),
            vmem((count, block, piece), BF16),
            vmem((count, block, piece), BF16),
            vmem((lot, piece), BF16),
            vmem((lot, piece), BF16),
            vmem((lot, count * block), BF16),
            vmem((lot, count * block), BF16),
            vmem((CHUNKS, count, lot, block), F32),
            vmem((CHUNKS, count, lot // 2, block), F32),
            vmem((CHUNKS, 3, count, lot // 8, block), F32),
            vmem((CHUNKS, count, lot // 8, block), F32),
            vmem((CHUNKS, 3, count, lot // 32, block), F32),
            vmem((CHUNKS, count, lot, block), F32),
            vmem((3, block, block), F32),
            vmem((7, 3, block // 8, block), F32),
            vmem((3, block // 8, block), F32),
            vmem((3, 3, block // 8, block), F32),
            vmem((8, 3, block // 8, block), F32),
            vmem((count, 3, block, block), F32),
            vmem((count * block, count * block), BF16),
            vmem((count * block, count * block), BF16),
            dma((CHUNKS, 3)),
            dma((CHUNKS, 3)),
            dma((CHUNKS,)),
            dma((CHUNKS,)),
            dma((7,)),
            dma((7,)),
            dma,
            dma((5, 8)),
            dma((5, 8)),
            dma((CHUNKS, 14)),
            dma((CHUNKS, 14)),
        ],
        compiler_params=pltpu.CompilerParams(
            collective_id=1, has_side_effects=True, vmem_limit_bytes=60 * 2**20
        ),
    )(vectors, reflectors, factors)
    return out.reshape(rows * 32, piece)


def solution(mesh):
    placed = (P(("row", "col"), None), P(None, "col", "row"), P())
    return jax.shard_map(
        on_device, mesh=mesh, in_specs=placed, out_specs=P("col", "row"), check_vma=False
    )
```

time: 502 us -> 241 us (0.48)
  the two profiles are of different devices: /device:TPU:5 before, /device:TPU:39 now
where the time goes in v2:
time: 241 us
  Pallas kernels  236 us (98%)
  local copies, waits for them, and re-layouts  4.79 us (2%)
    pallas_call x1, Pallas kernels, on_device(): pl.pallas_call(kernel, out_shape=jax.ShapeDtypeStruct((32, CHUNKS, rows /...  236 us

profile of v2, /device:TPU:39, one launch (start us, length us, event | category | flops | bytes accessed | tf_op | source)
XLA Modules:
  0.0 241.2 jit_solution(5139674603536122432)
XLA Ops:
  0.0 236.4 %shard_map.37 = f32[32,4,8,1024]{3,2,1,0:T(8,128)} custom-call(f32[32,32768]{1,0:T(8,128)} %vec.1, f32[6,16,1024]{2,1,0:T(8,128)} %refl.1, f32[6,128,128]{2,1,0:T(8,128)} %factors.1), custom_call_target="tpu_custom_call" | custom-call | tf_op jit(solution)/shard_map/pallas_call | solution.py:346
  236.4 4.8 %copy.5 = f32[1024,1024]{1,0:T(8,128)} copy(f32[1024,1024]{1,0:T(8,128)} %bitcast.1) | data formatting | bytes 8388608

commit v3 on v2

--- a/solution.py
+++ b/solution.py
@@ -31,15 +31,14 @@
 
 def kernel(
     vec, refl, factors, out,
-    x, held, panels, vh, vl, xh, xl, uh, ul, proj, r1, r2, s2, r3, upd,
+    x, held, turned, passed, panels, vh, vl, xh, xl, uh, ul, proj, r1, r2, s2, r3, upd,
     gp, g1, gs, g2, gc, gall, th, tl,
-    sent_a, came_a, sent_b, came_b, sent_v, came_v, own_v, sent_g, came_g, sent_p, came_p,
+    sent_a, came_a, sent_t, came_t, sent_r, came_r, sent_b, came_b, sent_v, came_v, own_v, sent_g, came_g, sent_p, came_p,
 ):
     row, col = lax.axis_index("row"), lax.axis_index("col")
     y, near = row // 8, row % 8
     zh, core = near // 2, near % 2
     far_x, zl = col // 2, col % 2
-    slot = (near % 4) * 8 + col
     upper = near // 4
     count, block, piece = panels.shape
     own = refl.shape[1]
@@ -73,27 +72,18 @@
 
     barrier = pltpu.get_barrier_semaphore()
     greeted = []
-    for k in range(4):
-        for w in range(8):
-            greeted.append((y * 8 + w, k * 2 + upper))
-    for w in range(4):
-        for c in range(8):
-            greeted.append((y * 8 + zl * 4 + w, c))
+    for w in range(8):
+        greeted.append((y * 8 + w, far_x * 2 + upper))
+        greeted.append((y * 8 + zl * 4 + w // 2, far_x * 2 + w % 2))
     for o in range(1, 8):
         greeted.append(at((y + o // 2) % 4, zh, (core + o) % 2, col))
         greeted.append((row, (col + o) % 8))
     for k in range(1, 4):
         greeted.append(in_z(k))
+        greeted.append(at(y, (zh + k) % 4, 1 - core, col))
     for device in greeted:
         pl.semaphore_signal(barrier, inc=1, device_id=device, device_id_type=MESH)
     pl.semaphore_wait(barrier, len(greeted))
-
-    mine = panels.at[:, part(col, own), :]
-    others = panels.at[:, part(far_x * 2 + 1 - zl, own), :]
-    keep = pltpu.make_async_copy(refl, mine, own_v)
-    keep.start()
-    beside = send(refl, mine, sent_v.at[0], came_v.at[0], (row, far_x * 2 + 1 - zl))
-    from_x = [send(refl, mine, sent_v.at[k], came_v.at[k], in_x(k)) for k in (1, 3, 2)]
 
     first = {}
     for c in range(CHUNKS):
@@ -103,38 +93,103 @@
                 sent_a.at[c, k - 1], came_a.at[c, k - 1], in_y(k),
             )
 
-    local = zl == upper
-
-    def second(c):
+    mine = panels.at[:, part(col, own), :]
+    others = panels.at[:, part(far_x * 2 + 1 - zl, own), :]
+    keep = pltpu.make_async_copy(refl, mine, own_v)
+    keep.start()
+    beside = send(refl, mine, sent_v.at[0], came_v.at[0], (row, far_x * 2 + 1 - zl))
+
+    def turn(c):
         for k in (0, 1, 3, 2):
             if k:
                 first[c, k].wait_recv()
-            there = ((y - k) % 4) * 2 + upper
-            for flip in range(2):
-                for j in (1, 3, 2, 0):
+            origin = (y - k) % 4
+            source = held.at[c, k - 1] if k else vec.at[pl.ds(c * 8, 8), part(y, 8 * piece)]
+            there = (origin - far_x) % 4
+            target = turned.at[c, there]
+            sem = came_t.at[c, there]
+
+            @pl.when(origin == far_x)
+            def _():
+                pltpu.make_async_copy(source, target, sem).start()
+
+            @pl.when(origin != far_x)
+            def _():
+                remote(source, target, sent_t.at[c], sem, (row, origin * 2 + zl)).start()
+
+    local = zl == upper
+
+    def slot(from_zh, k):
+        return ((from_zh % 2) * 2 + core) * 8 + ((far_x - k) % 4) * 2 + zl
+
+    def way(half):
+        if half:
+            return jnp.where(zh == 3, 1, 3)
+        return jnp.where(zh == 0, 3, 1)
+
+    def second(c):
+        for k in (0, 1, 3, 2):
+            remote(
+                turned.at[c, k], turned.at[c, k], sent_t.at[c], came_t.at[c, k], (row, col)
+            ).wait_recv()
+            target = x.at[c, part(slot(zh, k), 8), :]
+            for j in (2, 1, 3, 0):
+                for flip in range(2):
                     to_zh, to_core = (zh + j) % 4, (core + flip) % 2
-                    w = to_zh * 2 + to_core
-                    if k:
-                        source = held.at[c, k - 1, :, part(w, piece)]
+                    source = turned.at[c, k, :, part(to_zh * 2 + to_core, piece)]
+                    device = at(y, to_zh, to_core, far_x * 2 + upper)
+                    if j == 0 and flip == 0 or j == 2:
+
+                        @pl.when(local)
+                        def _():
+                            if j == 0:
+                                pltpu.make_async_copy(source, target, came_b.at[c]).start()
+                            else:
+                                remote(
+                                    source, passed.at[c, flip, k], sent_b.at[c], came_r.at[c, flip],
+                                    at(y, (zh + way(flip)) % 4, core, far_x * 2 + upper),
+                                ).start()
+
+                        @pl.when(jnp.logical_not(local))
+                        def _():
+                            remote(source, target, sent_b.at[c], came_b.at[c], device).start()
+
                     else:
-                        source = vec.at[pl.ds(c * 8, 8), part(y * 8 + w, piece)]
-                    target = x.at[c, part(slot, 8), :]
-                    copy = remote(source, target, sent_b.at[c], came_b.at[c], at(y, to_zh, to_core, there))
-                    if flip or j:
-                        copy.start()
-                    else:
-
-                        @pl.when(there == col)
-                        def _(source=source, target=target):
-                            pltpu.make_async_copy(source, target, came_b.at[c]).start()
-
-                        @pl.when(there != col)
-                        def _(copy=copy):
-                            copy.start()
-
+                        remote(source, target, sent_b.at[c], came_b.at[c], device).start()
+
+    from_zh = jnp.where(zl == 0, jnp.where(zh == 3, 0, 1), jnp.where(zh == 0, 3, 2))
+    passes = (
+        jnp.where(zl == 0, jnp.where(zh >= 2, 1, 0), jnp.where((zh + 1) % 4 <= 1, 1, 0)) == 1,
+        jnp.where(zl == 0, jnp.where((zh + 1) % 4 <= 1, 1, 0), jnp.where(zh <= 1, 1, 0)) == 1,
+    )
+
+    def relay(c):
+        for half in range(2):
+
+            @pl.when(passes[half])
+            def _():
+                whole = passed.at[c, half]
+                remote(whole, whole, sent_r.at[c, half], came_r.at[c, half], (row, col)).wait_recv()
+                for k in (0, 1, 3, 2):
+                    remote(
+                        passed.at[c, half, k], x.at[c, part(slot(from_zh, k), 8), :],
+                        sent_r.at[c, half], came_b.at[c],
+                        at(y, (from_zh + 2) % 4, (core + half) % 2, col),
+                    ).start()
+
+    turn(0)
     second(0)
+    from_x = [send(refl, mine, sent_v.at[k], came_v.at[k], in_x(k)) for k in (1, 3, 2)]
+    turn(1)
+    relay(0)
+    turn(2)
     beside.wait_recv()
     from_z = [send(others, others, sent_v.at[3 + k], came_v.at[3 + k], in_x(k)) for k in (1, 3, 2)]
+    second(1)
+    relay(1)
+    turn(3)
+    second(2)
+    relay(2)
     for copy in from_x + from_z:
         copy.wait_recv()
     keep.wait()
@@ -156,17 +211,17 @@
                 sent_g.at[0, o], came_g.at[0, o], at(to_y, zh, to_core, col),
             )
         )
-    second(1)
-    for copy in step_1:
-        copy.wait_recv()
-    total = gp[:, part(core * 4 + y, lot), :]
-    for o in range(7):
-        total = total + g1[o]
-    gs[...] = total
-    step_2 = [send(gs, g2.at[k - 1], sent_g.at[1, k], came_g.at[1, k], in_z(k)) for k in (1, 3, 2)]
-
-    def g_col():
-        for copy in step_2:
+    def g_sum():
+        for copy in step_1:
+            copy.wait_recv()
+        total = gp[:, part(core * 4 + y, lot), :]
+        for o in range(7):
+            total = total + g1[o]
+        gs[...] = total
+        return [send(gs, g2.at[k - 1], sent_g.at[1, k], came_g.at[1, k], in_z(k)) for k in (1, 3, 2)]
+
+    def g_col(before):
+        for copy in before:
             copy.wait_recv()
         gc[col] = gs[...] + g2[0] + (g2[1] + g2[2])
         return [
@@ -294,43 +349,55 @@
 
         lax.fori_loop(0, piece // wide, tile, 0)
 
-    state = {}
-    g = None
-    for c in range(CHUNKS + 2):
-        if c < CHUNKS:
-            state[c] = project(c)
-        if c == 0:
-            g = g_col()
-        if c == 1:
-            whole_factor(g)
-        if 0 <= c - 1 < CHUNKS:
-            state[c - 1] = update(c - 1, state[c - 1])
-        if c < CHUNKS:
-            state[c] = sum_core(c, state[c])
-        if c == 0:
-            g = g_y(g)
-        if 0 <= c - 2 < CHUNKS:
-            state[c - 2] = all_z(c - 2, state[c - 2])
-        if c < CHUNKS:
-            state[c] = sum_y(c, state[c])
-        if c == 0:
-            g = g_core(g)
-        if c + 2 < CHUNKS:
-            second(c + 2)
-        if 0 <= c - 2 < CHUNKS:
-            state[c - 2] = all_y(c - 2, state[c - 2])
-            finish(c - 2, state[c - 2])
+    at_0, at_1 = project(0), project(1)
+    g = g_sum()
+    at_0, at_1 = sum_core(0, at_0), sum_core(1, at_1)
+    at_0, at_1 = sum_y(0, at_0), sum_y(1, at_1)
+    g = g_col(g)
+    second(3)
+    relay(3)
+    at_2 = project(2)
+    g = g_y(g)
+    at_2 = sum_core(2, at_2)
+    g = g_core(g)
+    at_2 = sum_y(2, at_2)
+    whole_factor(g)
+    at_0, at_1 = update(0, at_0), update(1, at_1)
+    at_3 = project(3)
+    at_2 = update(2, at_2)
+    at_3 = sum_core(3, at_3)
+    at_0, at_1 = all_z(0, at_0), all_z(1, at_1)
+    at_3 = sum_y(3, at_3)
+    at_2 = all_z(2, at_2)
+    at_0, at_1 = all_y(0, at_0), all_y(1, at_1)
+    at_3 = update(3, at_3)
+    finish(0, at_0)
+    at_3 = all_z(3, at_3)
+    at_2 = all_y(2, at_2)
+    finish(1, at_1)
+    at_3 = all_y(3, at_3)
+    finish(2, at_2)
+    finish(3, at_3)
 
     for c in range(CHUNKS):
+        three = turned.at[c, pl.ds(0, 3)]
+        remote(three, three, sent_t.at[c], came_t.at[c, 0], (row, col)).wait_send()
 
         @pl.when(local)
         def _():
-            some = x.at[c, pl.ds(0, x.shape[1] - 8), :]
+            some = x.at[c, pl.ds(0, x.shape[1] - 32), :]
             remote(some, some, sent_b.at[c], came_b.at[c], (row, col)).wait_send()
 
         @pl.when(jnp.logical_not(local))
         def _():
             remote(x.at[c], x.at[c], sent_b.at[c], came_b.at[c], (row, col)).wait_send()
+
+        for half in range(2):
+
+            @pl.when(passes[half])
+            def _():
+                whole = passed.at[c, half]
+                remote(whole, whole, sent_r.at[c, half], came_r.at[c, half], (row, col)).wait_send()
 
     for copy in pending:
         copy.wait_send()
@@ -345,7 +412,7 @@
     dma = pltpu.SemaphoreType.DMA
     out = pl.pallas_call(
         kernel,
-        out_shape=jax.ShapeDtypeStruct((32, CHUNKS, rows // CHUNKS, piece), F32),
+        out_shape=vmem((32, CHUNKS, rows // CHUNKS, piece), F32),
         in_specs=[
             pl.BlockSpec(memory_space=pl.ANY),
             pl.BlockSpec(memory_space=pl.ANY),
@@ -355,6 +422,8 @@
         scratch_shapes=[
             vmem((CHUNKS, lot, piece), F32),
             vmem((CHUNKS, 3, 8, 8 * piece), F32),
+            vmem((CHUNKS, 4, 8, 8 * piece), F32),
+            vmem((CHUNKS, 2, 4, 8, piece), F32),
             vmem((count, block, piece), F32),
             vmem((count, block, piece), BF16),
             vmem((count, block, piece), BF16),
@@ -379,6 +448,10 @@
             dma((CHUNKS, 3)),
             dma((CHUNKS, 3)),
             dma((CHUNKS,)),
+            dma((CHUNKS, 4)),
+            dma((CHUNKS, 2)),
+            dma((CHUNKS, 2)),
+            dma((CHUNKS,)),
             dma((CHUNKS,)),
             dma((7,)),
             dma((7,)),
@@ -389,7 +462,7 @@
             dma((CHUNKS, 14)),
         ],
         compiler_params=pltpu.CompilerParams(
-            collective_id=1, has_side_effects=True, vmem_limit_bytes=60 * 2**20
+            collective_id=1, has_side_effects=True, vmem_limit_bytes=52 * 2**20
         ),
     )(vectors, reflectors, factors)
     return out.reshape(rows * 32, piece)

time: 241 us -> 208 us (0.86)
  Pallas kernels: 236 us -> 205 us
  local copies, waits for them, and re-layouts: 4.79 us -> 2.02 us
    pallas_call x1, Pallas kernels: 236 us -> 205 us  [on_device(): pl.pallas_call(kernel, out_shape=vmem((32, CHUNKS, rows // CHUNKS, piece)...]
    unnamed x1, local copies, waits for them, and re-layouts: 4.79 us -> 2.02 us
where the time goes in v3:
time: 208 us; the launch traced here: 207 us
  Pallas kernels  205 us (99%)
    pallas_call x1, Pallas kernels, on_device(): pl.pallas_call(kernel, out_shape=vmem((32, CHUNKS, rows // CHUNKS, piece)...  205 us

profile of v3, /device:TPU:39, one launch (start us, length us, event | category | flops | bytes accessed | tf_op | source)
XLA Modules:
  0.0 206.8 jit_solution(14925108396802819256)
XLA Ops:
  0.0 204.8 %shard_map.37 = f32[32,4,8,1024]{3,2,1,0:T(8,128)S(1)} custom-call(f32[32,32768]{1,0:T(8,128)} %vec.1, f32[6,16,1024]{2,1,0:T(8,128)} %refl.1, f32[6,128,128]{2,1,0:T(8,128)} %factors.1), custom_call_target="tpu_custom_call" | custom-call | tf_op jit(solution)/shard_map/pallas_call | solution.py:413
  204.8 2.0 copy.5

commit v4 on v3

--- a/solution.py
+++ b/solution.py
@@ -9,6 +9,7 @@
 BF16 = jnp.bfloat16
 MESH = pl.DeviceIdType.MESH
 CHUNKS = 4
+LAST = CHUNKS - 1
 NT = (((1,), (1,)), ((), ()))
 NN = (((1,), (0,)), ((), ()))
 
@@ -31,9 +32,10 @@
 
 def kernel(
     vec, refl, factors, out,
-    x, held, turned, passed, panels, vh, vl, xh, xl, uh, ul, proj, r1, r2, s2, r3, upd,
+    x, held, turned, passed, early, risen, passed_early, panels, vh, vl, xh, xl, uh, ul, proj, r1, r2, s2, r3, upd,
     gp, g1, gs, g2, gc, gall, th, tl,
-    sent_a, came_a, sent_t, came_t, sent_r, came_r, sent_b, came_b, sent_v, came_v, own_v, sent_g, came_g, sent_p, came_p,
+    sent_a, came_a, sent_t, came_t, sent_r, came_r, sent_b, came_b,
+    sent_e, came_e, sent_pe, came_pe, sent_u, came_u, sent_v, came_v, own_v, sent_g, came_g, sent_p, came_p,
 ):
     row, col = lax.axis_index("row"), lax.axis_index("col")
     y, near = row // 8, row % 8
@@ -81,17 +83,21 @@
     for k in range(1, 4):
         greeted.append(in_z(k))
         greeted.append(at(y, (zh + k) % 4, 1 - core, col))
+        greeted.append((row + 1 - 2 * core, ((far_x + k) % 4) * 2 + zl))
     for device in greeted:
         pl.semaphore_signal(barrier, inc=1, device_id=device, device_id_type=MESH)
     pl.semaphore_wait(barrier, len(greeted))
 
     first = {}
-    for c in range(CHUNKS):
+
+    def begin(c):
         for k in (1, 3, 2):
             first[c, k] = send(
                 vec.at[pl.ds(c * 8, 8), part((y + k) % 4, 8 * piece)], held.at[c, k - 1],
                 sent_a.at[c, k - 1], came_a.at[c, k - 1], in_y(k),
             )
+
+    begin(0)
 
     mine = panels.at[:, part(col, own), :]
     others = panels.at[:, part(far_x * 2 + 1 - zl, own), :]
@@ -127,8 +133,8 @@
             return jnp.where(zh == 3, 1, 3)
         return jnp.where(zh == 0, 3, 1)
 
-    def second(c):
-        for k in (0, 1, 3, 2):
+    def second(c, steps=(0, 1, 3, 2)):
+        for k in steps:
             remote(
                 turned.at[c, k], turned.at[c, k], sent_t.at[c], came_t.at[c, k], (row, col)
             ).wait_recv()
@@ -177,19 +183,93 @@
                         at(y, (from_zh + 2) % 4, (core + half) % 2, col),
                     ).start()
 
+    def early_z():
+        for j in (2, 1, 3, 0):
+            for k in range(4):
+                to_y, to_zh = (y + k) % 4, (zh + j) % 4
+                source = vec.at[pl.ds(LAST * 8, 8), part(to_y * 4 + to_zh, 2 * piece)]
+                target = early.at[to_y, (zh % 2) * 2 + zl]
+                device = at(y, to_zh, core, far_x * 2 + upper)
+                if j % 2:
+                    remote(source, target, sent_e, came_e, device).start()
+                else:
+
+                    @pl.when(local)
+                    def _():
+                        if j == 0:
+                            pltpu.make_async_copy(source, target, came_e).start()
+                        else:
+                            remote(
+                                source, passed_early.at[k // 2, k % 2], sent_e, came_pe.at[k // 2],
+                                at(y, (zh + way(k // 2)) % 4, core, far_x * 2 + upper),
+                            ).start()
+
+                    @pl.when(jnp.logical_not(local))
+                    def _():
+                        remote(source, target, sent_e, came_e, device).start()
+
+    def early_relay():
+        for half in range(2):
+
+            @pl.when(passes[half])
+            def _():
+                whole = passed_early.at[half]
+                remote(whole, whole, sent_pe.at[half], came_pe.at[half], (row, col)).wait_recv()
+                for i in range(2):
+                    remote(
+                        passed_early.at[half, i], early.at[(y + half * 2 + i) % 4, (from_zh % 2) * 2 + zl],
+                        sent_pe.at[half], came_e, at(y, (from_zh + 2) % 4, core, col),
+                    ).start()
+
+    def early_y():
+        remote(early, early, sent_e, came_e, (row, col)).wait_recv()
+        return {
+            k: send(
+                early.at[(y + k) % 4], risen.at[k - 1], sent_u.at[k - 1], came_u.at[k - 1], in_y(k)
+            )
+            for k in (1, 3, 2)
+        }
+
+    def early_x(before):
+        for k in (0, 1, 3, 2):
+            if k:
+                before[k].wait_recv()
+            origin = (y - k) % 4
+            for q in range(4):
+                for flip in range(2):
+                    to_core = (core + flip) % 2
+                    lanes = part(to_core, piece)
+                    source = risen.at[k - 1, q, :, lanes] if k else early.at[y, q, :, lanes]
+                    place = (q // 2 * 2 + core) * 8 + far_x * 2 + q % 2
+                    target = x.at[LAST, part(place, 8), :]
+                    there = remote(
+                        source, target, sent_b.at[LAST], came_b.at[LAST], at(y, zh, to_core, origin * 2 + zl)
+                    )
+                    if flip:
+                        there.start()
+                    else:
+
+                        @pl.when(origin == far_x)
+                        def _():
+                            pltpu.make_async_copy(source, target, came_b.at[LAST]).start()
+
+                        @pl.when(origin != far_x)
+                        def _():
+                            there.start()
+
+    early_z()
+    begin(1)
+    begin(2)
     turn(0)
+    from_x = [send(refl, mine, sent_v.at[k], came_v.at[k], in_x(k)) for k in (1, 3, 2)]
+    early_relay()
     second(0)
-    from_x = [send(refl, mine, sent_v.at[k], came_v.at[k], in_x(k)) for k in (1, 3, 2)]
+    beside.wait_recv()
+    from_z = [send(others, others, sent_v.at[3 + k], came_v.at[3 + k], in_x(k)) for k in (1, 3, 2)]
     turn(1)
     relay(0)
     turn(2)
-    beside.wait_recv()
-    from_z = [send(others, others, sent_v.at[3 + k], came_v.at[3 + k], in_x(k)) for k in (1, 3, 2)]
-    second(1)
-    relay(1)
-    turn(3)
-    second(2)
-    relay(2)
+    rising = early_y()
     for copy in from_x + from_z:
         copy.wait_recv()
     keep.wait()
@@ -349,37 +429,47 @@
 
         lax.fori_loop(0, piece // wide, tile, 0)
 
-    at_0, at_1 = project(0), project(1)
+    at_0 = project(0)
     g = g_sum()
-    at_0, at_1 = sum_core(0, at_0), sum_core(1, at_1)
-    at_0, at_1 = sum_y(0, at_0), sum_y(1, at_1)
+    second(1, (0, 1))
     g = g_col(g)
-    second(3)
-    relay(3)
+    second(1, (3, 2))
+    at_0 = sum_core(0, at_0)
+    relay(1)
+    at_0 = sum_y(0, at_0)
+    early_x(rising)
+    second(2)
+    g = g_y(g)
+    at_3 = project(3)
+    g = g_core(g)
+    at_1 = project(1)
+    at_3 = sum_core(3, at_3)
+    whole_factor(g)
+    at_0 = update(0, at_0)
+    at_1 = sum_core(1, at_1)
+    at_3 = sum_y(3, at_3)
+    at_1 = sum_y(1, at_1)
+    relay(2)
     at_2 = project(2)
-    g = g_y(g)
+    at_3 = update(3, at_3)
     at_2 = sum_core(2, at_2)
-    g = g_core(g)
+    at_1 = update(1, at_1)
+    at_0 = all_z(0, at_0)
+    at_3 = all_z(3, at_3)
     at_2 = sum_y(2, at_2)
-    whole_factor(g)
-    at_0, at_1 = update(0, at_0), update(1, at_1)
-    at_3 = project(3)
+    at_1 = all_z(1, at_1)
+    at_0 = all_y(0, at_0)
     at_2 = update(2, at_2)
-    at_3 = sum_core(3, at_3)
-    at_0, at_1 = all_z(0, at_0), all_z(1, at_1)
-    at_3 = sum_y(3, at_3)
+    at_3 = all_y(3, at_3)
+    finish(0, at_0)
     at_2 = all_z(2, at_2)
-    at_0, at_1 = all_y(0, at_0), all_y(1, at_1)
-    at_3 = update(3, at_3)
-    finish(0, at_0)
-    at_3 = all_z(3, at_3)
+    at_1 = all_y(1, at_1)
+    finish(3, at_3)
     at_2 = all_y(2, at_2)
     finish(1, at_1)
-    at_3 = all_y(3, at_3)
     finish(2, at_2)
-    finish(3, at_3)
-
-    for c in range(CHUNKS):
+
+    for c in range(LAST):
         three = turned.at[c, pl.ds(0, 3)]
         remote(three, three, sent_t.at[c], came_t.at[c, 0], (row, col)).wait_send()
 
@@ -398,6 +488,25 @@
             def _():
                 whole = passed.at[c, half]
                 remote(whole, whole, sent_r.at[c, half], came_r.at[c, half], (row, col)).wait_send()
+
+    sent = x.at[LAST, pl.ds(0, x.shape[1] - 32), :]
+    remote(sent, sent, sent_b.at[LAST], came_b.at[LAST], (row, col)).wait_send()
+
+    @pl.when(local)
+    def _():
+        some = early.at[pl.ds(0, 3)]
+        remote(some, some, sent_e, came_e, (row, col)).wait_send()
+
+    @pl.when(jnp.logical_not(local))
+    def _():
+        remote(early, early, sent_e, came_e, (row, col)).wait_send()
+
+    for half in range(2):
+
+        @pl.when(passes[half])
+        def _():
+            whole = passed_early.at[half]
+            remote(whole, whole, sent_pe.at[half], came_pe.at[half], (row, col)).wait_send()
 
     for copy in pending:
         copy.wait_send()
@@ -421,9 +530,12 @@
         out_specs=pl.BlockSpec(memory_space=vmem),
         scratch_shapes=[
             vmem((CHUNKS, lot, piece), F32),
-            vmem((CHUNKS, 3, 8, 8 * piece), F32),
-            vmem((CHUNKS, 4, 8, 8 * piece), F32),
-            vmem((CHUNKS, 2, 4, 8, piece), F32),
+            vmem((LAST, 3, 8, 8 * piece), F32),
+            vmem((LAST, 4, 8, 8 * piece), F32),
+            vmem((LAST, 2, 4, 8, piece), F32),
+            vmem((4, 4, 8, 2 * piece), F32),
+            vmem((3, 4, 8, 2 * piece), F32),
+            vmem((2, 2, 8, 2 * piece), F32),
             vmem((count, block, piece), F32),
             vmem((count, block, piece), BF16),
             vmem((count, block, piece), BF16),
@@ -453,6 +565,12 @@
             dma((CHUNKS, 2)),
             dma((CHUNKS,)),
             dma((CHUNKS,)),
+            dma,
+            dma,
+            dma((2,)),
+            dma((2,)),
+            dma((3,)),
+            dma((3,)),
             dma((7,)),
             dma((7,)),
             dma,

time: 208 us -> 189 us (0.909); the launches traced: 207 us -> 186 us
  Pallas kernels: 205 us -> 184 us
    pallas_call x1, Pallas kernels: 205 us -> 184 us  [on_device(): pl.pallas_call(kernel, out_shape=vmem((32, CHUNKS, rows // CHUNKS, piece)...]
where the time goes in v4:
time: 189 us; the launch traced here: 186 us
  Pallas kernels  184 us (97%)
  local copies, waits for them, and re-layouts  2.02 us (1%)
    pallas_call x1, Pallas kernels, on_device(): pl.pallas_call(kernel, out_shape=vmem((32, CHUNKS, rows // CHUNKS, piece)...  184 us

profile of v4, /device:TPU:39, one launch (start us, length us, event | category | flops | bytes accessed | tf_op | source)
XLA Modules:
  0.0 185.6 jit_solution(16590765775631742685)
XLA Ops:
  0.0 183.6 %shard_map.37 = f32[32,4,8,1024]{3,2,1,0:T(8,128)S(1)} custom-call(f32[32,32768]{1,0:T(8,128)} %vec.1, f32[6,16,1024]{2,1,0:T(8,128)} %refl.1, f32[6,128,128]{2,1,0:T(8,128)} %factors.1), custom_call_target="tpu_custom_call" | custom-call | tf_op jit(solution)/shard_map/pallas_call | solution.py:522
  183.6 2.0 %copy.5 = f32[1024,1024]{1,0:T(8,128)} copy(f32[1024,1024]{1,0:T(8,128)S(1)} %bitcast.1) | data formatting | bytes 8388608

commit v5 on v4

--- a/solution.py
+++ b/solution.py
@@ -133,35 +133,41 @@
             return jnp.where(zh == 3, 1, 3)
         return jnp.where(zh == 0, 3, 1)
 
-    def second(c, steps=(0, 1, 3, 2)):
+    def second(c, steps=(0, 1, 3, 2), opposite=True):
+        def go(k, j):
+            target = x.at[c, part(slot(zh, k), 8), :]
+            for flip in range(2):
+                to_zh, to_core = (zh + j) % 4, (core + flip) % 2
+                source = turned.at[c, k, :, part(to_zh * 2 + to_core, piece)]
+                device = at(y, to_zh, to_core, far_x * 2 + upper)
+                if j == 0 and flip == 0 or j == 2:
+
+                    @pl.when(local)
+                    def _():
+                        if j == 0:
+                            pltpu.make_async_copy(source, target, came_b.at[c]).start()
+                        else:
+                            remote(
+                                source, passed.at[c, flip, k], sent_b.at[c], came_r.at[c, flip],
+                                at(y, (zh + way(flip)) % 4, core, far_x * 2 + upper),
+                            ).start()
+
+                    @pl.when(jnp.logical_not(local))
+                    def _():
+                        remote(source, target, sent_b.at[c], came_b.at[c], device).start()
+
+                else:
+                    remote(source, target, sent_b.at[c], came_b.at[c], device).start()
+
+        if opposite:
+            for k in (0, 1, 3, 2):
+                remote(
+                    turned.at[c, k], turned.at[c, k], sent_t.at[c], came_t.at[c, k], (row, col)
+                ).wait_recv()
+                go(k, 2)
         for k in steps:
-            remote(
-                turned.at[c, k], turned.at[c, k], sent_t.at[c], came_t.at[c, k], (row, col)
-            ).wait_recv()
-            target = x.at[c, part(slot(zh, k), 8), :]
-            for j in (2, 1, 3, 0):
-                for flip in range(2):
-                    to_zh, to_core = (zh + j) % 4, (core + flip) % 2
-                    source = turned.at[c, k, :, part(to_zh * 2 + to_core, piece)]
-                    device = at(y, to_zh, to_core, far_x * 2 + upper)
-                    if j == 0 and flip == 0 or j == 2:
-
-                        @pl.when(local)
-                        def _():
-                            if j == 0:
-                                pltpu.make_async_copy(source, target, came_b.at[c]).start()
-                            else:
-                                remote(
-                                    source, passed.at[c, flip, k], sent_b.at[c], came_r.at[c, flip],
-                                    at(y, (zh + way(flip)) % 4, core, far_x * 2 + upper),
-                                ).start()
-
-                        @pl.when(jnp.logical_not(local))
-                        def _():
-                            remote(source, target, sent_b.at[c], came_b.at[c], device).start()
-
-                    else:
-                        remote(source, target, sent_b.at[c], came_b.at[c], device).start()
+            for j in (1, 3, 0):
+                go(k, j)
 
     from_zh = jnp.where(zl == 0, jnp.where(zh == 3, 0, 1), jnp.where(zh == 0, 3, 2))
     passes = (
@@ -395,7 +401,15 @@
             copy.wait_recv()
         total = s2[c, :, part(zh, 8), :] + r3[c, 0] + (r3[c, 1] + r3[c, 2])
         flat = jnp.concatenate([total[k] for k in range(count)], axis=1)
-        value = dot3(halves(flat), (th[...], tl[...]), NT)
+        high, low = halves(flat)
+        stack = jnp.concatenate([high.astype(F32), low.astype(F32)], axis=0).astype(BF16)
+        values = []
+        for p in range(0, count, 2):
+            lines, rest = pl.ds(p * block, 2 * block), pl.ds(p * block, (count - p) * block)
+            both = lax.dot_general(stack[:, p * block :], th[lines, rest], NT, preferred_element_type=F32)
+            less = lax.dot_general(high[:, p * block :], tl[lines, rest], NT, preferred_element_type=F32)
+            values.append(both[:8] + (both[8:] + less))
+        value = jnp.concatenate(values, axis=1)
         lines = part((core * 4 + y) * 4 + zh, 8)
         for k in range(count):
             upd[c, k, lines, :] = value[:, k * block : (k + 1) * block]
@@ -432,31 +446,31 @@
     at_0 = project(0)
     g = g_sum()
     second(1, (0, 1))
+    at_0 = sum_core(0, at_0)
     g = g_col(g)
-    second(1, (3, 2))
-    at_0 = sum_core(0, at_0)
-    relay(1)
     at_0 = sum_y(0, at_0)
+    second(1, (3, 2), False)
     early_x(rising)
     second(2)
+    relay(1)
+    at_3 = project(3)
     g = g_y(g)
-    at_3 = project(3)
+    at_3 = sum_core(3, at_3)
     g = g_core(g)
     at_1 = project(1)
-    at_3 = sum_core(3, at_3)
+    relay(2)
+    at_3 = sum_y(3, at_3)
     whole_factor(g)
+    at_1 = sum_core(1, at_1)
     at_0 = update(0, at_0)
-    at_1 = sum_core(1, at_1)
-    at_3 = sum_y(3, at_3)
     at_1 = sum_y(1, at_1)
-    relay(2)
     at_2 = project(2)
+    at_2 = sum_core(2, at_2)
     at_3 = update(3, at_3)
-    at_2 = sum_core(2, at_2)
     at_1 = update(1, at_1)
     at_0 = all_z(0, at_0)
+    at_2 = sum_y(2, at_2)
     at_3 = all_z(3, at_3)
-    at_2 = sum_y(2, at_2)
     at_1 = all_z(1, at_1)
     at_0 = all_y(0, at_0)
     at_2 = update(2, at_2)

time: 189 us -> 179 us (0.947); the launches traced: 186 us -> 179 us
  Pallas kernels: 184 us -> 177 us
    pallas_call x1, Pallas kernels: 184 us -> 177 us  [on_device(): pl.pallas_call(kernel, out_shape=vmem((32, CHUNKS, rows // CHUNKS, piece)...]
where the time goes in v5:
time: 179 us
  Pallas kernels  177 us (99%)
  local copies, waits for them, and re-layouts  2.02 us (1%)
    pallas_call x1, Pallas kernels, on_device(): pl.pallas_call(kernel, out_shape=vmem((32, CHUNKS, rows // CHUNKS, piece)...  177 us

profile of v5, /device:TPU:39, one launch (start us, length us, event | category | flops | bytes accessed | tf_op | source)
XLA Modules:
  0.0 178.6 jit_solution(14104205023075014573)
XLA Ops:
  0.0 176.6 %shard_map.37 = f32[32,4,8,1024]{3,2,1,0:T(8,128)S(1)} custom-call(f32[32,32768]{1,0:T(8,128)} %vec.1, f32[6,16,1024]{2,1,0:T(8,128)} %refl.1, f32[6,128,128]{2,1,0:T(8,128)} %factors.1), custom_call_target="tpu_custom_call" | custom-call | tf_op jit(solution)/shard_map/pallas_call | solution.py:536
  176.6 2.0 %copy.5 = f32[1024,1024]{1,0:T(8,128)} copy(f32[1024,1024]{1,0:T(8,128)S(1)} %bitcast.1) | data formatting | bytes 8388608
